TPU v7x, 256 devices: a whole 4x4x8 slice. The times are simulated.
256 devices in a mesh: pair: 32 (over z, x), aux: 8 (over y, core).
Axes of the slice: x: 4, y: 4, z: 8, core: 2. Of those that a mesh axis runs over, the one named last changes fastest.
Arguments:
- integrals: bfloat16 [98304, 12288], P('pair', 'aux'), may hold values from -0.15625 to 0.15625
- energy_gaps: float32 [98304], P('pair'), may hold values from 0.3 to 3
- trial_vectors: float32 [98304, 64], P('pair'), may hold values from -160 to 160
Outputs:
- sigma_vectors: float32 [98304, 64], P(('pair', 'aux'))
- subspace: float32 [64, 64], replicated
- residuals: float32 [98304, 64], P(('pair', 'aux'))
- residual_norms: float32 [64], replicated
All inputs are finite; a program needn't handle non-finite values.
Results may differ from a plain program's by a relative error of at most 0.0052.
Values may be sent and summed in bfloat16 or wider, within the bound.
A program may use at most 64 MiB of HBM per device.

v0:
```python
import jax
import jax.numpy as jnp
from jax import lax
from jax.sharding import Mesh
from jax.sharding import PartitionSpec as P

AUX = ("aux_0", "aux_1")
PAIR = ("pair_0", "pair_1")
PAIR_AUX = ("pair_0", "pair_1", "aux_0", "aux_1")


epsilon = 1e-06


def split_up(value, dim, size):
    lengths = value.shape
    parts = value.reshape(*lengths[:dim], size, lengths[dim] // size, *lengths[dim + 1 :])
    return jnp.moveaxis(parts, dim, 0)


def sent_and_summed(value, axis, dim):
    parts = split_up(value, dim, lax.axis_size(axis))
    arrived = lax.all_to_all(parts, axis, split_axis=0, concat_axis=0, tiled=True)
    return arrived.sum(axis=0)


def copy_for_each(value, axis):
    copies = jnp.broadcast_to(value, (lax.axis_size(axis), *value.shape))
    return lax.all_to_all(copies, axis, split_axis=0, concat_axis=0, tiled=True)


def laid_out(parts, dim):
    parts = jnp.moveaxis(parts, 0, dim)
    lengths = parts.shape
    return parts.reshape(*lengths[:dim], lengths[dim] * lengths[dim + 1], *lengths[dim + 2 :])


def gather_directly(value, axis, dim):
    parts = copy_for_each(value, axis)
    return laid_out(parts, dim)


def summed_on_arrival(value, axis, dim):
    size = lax.axis_size(axis)
    parts = lax.all_to_all(split_up(value, dim, size), axis, 0, 0, tiled=True)
    return jnp.sum(parts.astype(jnp.float32), axis=0)


def taken_together(value, axis):
    return copy_for_each(value, axis).sum(axis=0)


def one_axis_at_a_time(value, axes):
    far, near = axes
    nearer = taken_together(value, near)
    return taken_together(nearer, far)


def packed_total(arrays, axis):
    ends = [0]
    for a in arrays:
        ends.append(ends[-1] + a.size)
    running = one_axis_at_a_time(jnp.concatenate([a.ravel() for a in arrays]), axis)
    return tuple((running[b:e].reshape(a.shape) for a, b, e in zip(arrays, ends, ends[1:])))


def local(integrals, energy_gaps, trial_vectors):
    pair_rows = trial_vectors.shape[0]
    row_share = pair_rows // lax.axis_size(AUX)
    total_pairs = float(pair_rows * lax.axis_size(PAIR))
    trial_half = trial_vectors.astype(jnp.bfloat16)
    partial_value = lax.dot_general(
        integrals, trial_half, (((0,), (0,)), ((), ())), preferred_element_type=jnp.float32
    )
    shares = sent_and_summed(partial_value, PAIR, 0).astype(jnp.bfloat16)
    terms = jnp.dot(integrals, gather_directly(shares, PAIR, 0), preferred_element_type=jnp.float32)
    coupled = summed_on_arrival(terms.astype(jnp.bfloat16), AUX, 0)
    first_own = lax.axis_index(AUX) * row_share
    own_trial = lax.dynamic_slice_in_dim(trial_vectors, first_own, row_share, 0)
    own_gaps = lax.dynamic_slice_in_dim(energy_gaps, first_own, row_share, 0)
    sigma_rows = own_gaps[:, None] * own_trial + 2.0 * coupled
    products = lax.dot_general(
        own_trial,
        sigma_rows,
        (((0,), (0,)), ((), ())),
        precision=lax.Precision.HIGHEST,
        preferred_element_type=jnp.float32,
    )
    squares = jnp.sum(own_trial * own_trial, axis=0)
    sigma_sq = jnp.sum(sigma_rows * sigma_rows, axis=0)
    products, squares, sigma_sq = packed_total(
        (products, squares, sigma_sq), (("pair_0", "pair_1"), ("aux_0", "aux_1"))
    )
    subspace = products / total_pairs
    rayleigh = jnp.diagonal(subspace) / (squares / total_pairs + epsilon)
    residual_rows = sigma_rows - own_trial * rayleigh[None, :]
    residual_sq = sigma_sq - 2.0 * rayleigh * jnp.diagonal(products) + rayleigh * rayleigh * squares
    residual_norms = jnp.sqrt(residual_sq / total_pairs + epsilon)
    return (sigma_rows, subspace, residual_rows, residual_norms)


def solution(mesh):
    finer = Mesh(mesh.devices.reshape(8, 4, 4, 2), ("pair_0", "pair_1", "aux_0", "aux_1"))
    return jax.shard_map(
        local,
        mesh=finer,
        in_specs=(P(PAIR, AUX), P(PAIR), P(PAIR, None)),
        out_specs=(P(PAIR_AUX, None), P(), P(PAIR_AUX, None), P()),
        check_vma=False,
    )
```

profile of v0, /device:TPU:1, one launch (start us, length us, event | category | flops | bytes accessed | tf_op | source)
XLA Modules:
  0.0 110.8 jit_solution(3957253671500624351)
XLA Ops:
  0.6 6.5 %fusion = f32[1536,64]{1,0:T(8,128)S(1)} fusion(bf16[3072,1536]{1,0:T(8,128)(2,1)} %param.3, f32[3072,64]{0,1:T(8,128)} %param.5), kind=kOutput, calls=%fused_computation.5 | convolution fusion | flops 604176384 | bytes 10616832 | tf_op jit(solution)/shard_map/reshape | solution.py:17
  7.1 0.5 reshape.58
  7.6 25.5 %all_to_all.27 = f32[32,1,3072]{2,1,0:T(1,128)S(1)} all-to-all(f32[32,1,3072]{2,1,0:T(1,128)S(1)} %reshape.58), channel_id=1, replica_groups=mesh['pair_0'=8,'pair_1'=4,'aux_0'=4,'aux_1'=2] {'pair_0','pair_1'}, dimensions={0} | all-to-all | bytes 786432 | tf_op jit(solution)/shard_map/all_to_all | solution.py:23
  33.1 0.5 broadcast.62
  33.6 1.6 %reduce.2 = f32[32,3072]{1,0:T(8,128)S(1)} reduce(f32[32,1,3072]{2,1,0:T(1,128)S(1)} %all_to_all.27, f32[]{:T(128)} %broadcast.62), dimensions={1}, to_apply=%all_to_all.17.reduce_sub_computation | reduce | bytes 786436 | tf_op jit(solution)/shard_map/all_to_all | solution.py:23
  35.2 0.2 reshape.59
  35.4 0.1 reduce_sum.54
  35.5 0.1 broadcast_in_dim.17
  35.5 0.2 reshape.60
  35.8 14.8 %all_to_all.28 = bf16[32,2,1536]{2,1,0:T(2,128)(2,1)S(1)} all-to-all(bf16[32,2,1536]{2,1,0:T(2,128)(2,1)S(1)} %reshape.60), channel_id=1, replica_groups=mesh['pair_0'=8,'pair_1'=4,'aux_0'=4,'aux_1'=2] {'pair_0','pair_1'}, dimensions={0} | all-to-all | bytes 393216 | tf_op jit(solution)/shard_map/all_to_all | solution.py:29
  50.5 0.3 reshape.61
  50.8 6.7 %convolution_convert_fusion = bf16[64,3072]{1,0:T(8,128)(2,1)S(1)} fusion(bf16[1536,64]{1,0:T(8,128)(2,1)S(1)} %bitcast.14, bf16[3072,1536]{1,0:T(8,128)(2,1)} %param.3), kind=kOutput, calls=%fused_computation.2 | convolution fusion | flops 604176384 | bytes 10027008 | tf_op jit(solution)/shard_map/dot_general | solution.py:76
  57.5 0.8 copy.36
  58.3 7.5 %all-to-all-start.2 = ((bf16[8,384,64]{1,2,0:T(8,128)(2,1)}), bf16[8,384,64]{1,2,0:T(8,128)(2,1)S(1)}, u32[]{:S(2)}, u32[]{:S(2)}) async-start(bf16[8,384,64]{1,2,0:T(8,128)(2,1)} %bitcast.12), calls=%async_computation.2 | async-start | bytes 786432 | tf_op jit(solution)/shard_map/all_to_all | solution.py:45
  65.8 0.8 dynamic_slice.6
  66.5 6.9 %all-to-all-done.2 = bf16[8,384,64]{1,2,0:T(8,128)(2,1)S(1)} async-done(((bf16[8,384,64]{1,2,0:T(8,128)(2,1)}), bf16[8,384,64]{1,2,0:T(8,128)(2,1)S(1)}, u32[]{:S(2)}, u32[]{:S(2)}) %all-to-all-start.2) | async-done | bytes 393248 | tf_op jit(solution)/shard_map/all_to_all | solution.py:45
  73.5 0.1 convert_reduce_fusion
  73.5 1.0 multiply_reduce_fusion
  74.5 0.0 copy-start.1
  74.6 1.2 %fusion.2 = f32[64,64]{1,0:T(8,128)S(1)} fusion(f32[384,64]{0,1:T(8,128)S(1)} %get-tuple-element.7, f32[3072,64]{0,1:T(8,128)} %param.5, s32[]{:T(128)S(6)} %select_n.10), kind=kOutput, calls=%fused_computation.11 | convolution fusion | flops 18874368 | bytes 212996 | tf_op jit(solution)/shard_map/dot_general | solution.py:82
  75.7 0.1 reshape.44
  75.8 0.1 concatenate.8
  75.9 0.1 broadcast_in_dim.18
  76.0 8.9 %all_to_all.29 = f32[8,1,4224]{2,1,0:T(1,128)S(1)} all-to-all(f32[8,1,4224]{2,1,0:T(1,128)S(1)} %broadcast_in_dim.18), channel_id=1, replica_groups=mesh['pair_0'=8,'pair_1'=4,'aux_0'=4,'aux_1'=2] {'aux_0','aux_1'}, dimensions={0} | all-to-all | bytes 270336 | tf_op jit(solution)/shard_map/all_to_all | solution.py:29
  84.9 0.1 reduce_sum.58
  85.0 1.1 broadcast_in_dim.19
  86.0 3.9 %all-to-all-start.4 = ((f32[32,1,4224]{2,1,0:T(1,128)}), f32[32,1,4224]{2,1,0:T(1,128)S(1)}, u32[]{:S(2)}, u32[]{:S(2)}) async-start(f32[32,1,4224]{2,1,0:T(1,128)} %broadcast_in_dim.19), calls=%async_computation.4 | async-start | bytes 1081344 | tf_op jit(solution)/shard_map/all_to_all | solution.py:29
  89.9 16.6 %all-to-all-done.4 = f32[32,1,4224]{2,1,0:T(1,128)S(1)} async-done(((f32[32,1,4224]{2,1,0:T(1,128)}), f32[32,1,4224]{2,1,0:T(1,128)S(1)}, u32[]{:S(2)}, u32[]{:S(2)}) %all-to-all-start.4) | async-done | bytes 540704 | tf_op jit(solution)/shard_map/all_to_all | solution.py:29
  106.6 0.3 reduce_sum.59
  106.9 0.1 reshape.45
  107.0 0.0 copy-start
  107.0 0.8 gather_fusion.1
  107.8 0.8 gather_fusion
  108.6 0.6 add_sqrt_fusion
  109.2 1.6 %multiply_subtract_fusion = f32[384,64]{0,1:T(8,128)} fusion(f32[384,64]{0,1:T(8,128)S(1)} %get-tuple-element.7, f32[3072,64]{0,1:T(8,128)} %param.5, s32[]{:T(128)S(6)} %select_n.10, f32[64]{0:T(128)S(1)} %get-tuple-element.5), kind=kLoop, calls=%fused_computation.7 | loop fusion | flops 49152 | bytes 295172 | tf_op jit(solution)/shard_map/sub | solution.py:96
  110.8 0.0 copy-done.1
  110.8 0.0 copy-done
  (3 shorter events, 0.0 us)
Async XLA Ops:
  58.3 15.2 %all-to-all-start.2 = ((bf16[8,384,64]{1,2,0:T(8,128)(2,1)}), bf16[8,384,64]{1,2,0:T(8,128)(2,1)S(1)}, u32[]{:S(2)}, u32[]{:S(2)}) async-start(bf16[8,384,64]{1,2,0:T(8,128)(2,1)} %bitcast.12), calls=%async_computation.2 | async-start | bytes 786432 | tf_op jit(solution)/shard_map/all_to_all | solution.py:45
  74.5 36.3 %copy-start.1 = (f32[384,64]{0,1:T(8,128)}, f32[384,64]{0,1:T(8,128)S(1)}, u32[]{:S(2)}) copy-start(f32[384,64]{0,1:T(8,128)S(1)} %get-tuple-element.7) | copy-start | bytes 294916
  86.0 20.5 %all-to-all-start.4 = ((f32[32,1,4224]{2,1,0:T(1,128)}), f32[32,1,4224]{2,1,0:T(1,128)S(1)}, u32[]{:S(2)}, u32[]{:S(2)}) async-start(f32[32,1,4224]{2,1,0:T(1,128)} %broadcast_in_dim.19), calls=%async_computation.4 | async-start | bytes 1081344 | tf_op jit(solution)/shard_map/all_to_all | solution.py:29
  107.0 3.8 %copy-start = (f32[64,64]{1,0:T(8,128)}, f32[64,64]{1,0:T(8,128)S(1)}, u32[]{:S(2)}) copy-start(f32[64,64]{1,0:T(8,128)S(1)} %broadcast_multiply_fusion) | copy-start | bytes 49156
where the time goes:
time: 112 us; the launch traced here: 111 us
  blocking collectives  49.1 us (44%)
  waiting for transfers between devices  23.6 us (21%)
  matrix products  14.3 us (13%)
  starting transfers between devices  11.4 us (10%)
  local copies, waits for them, and re-layouts  6.32 us (6%)
  other arithmetic  5.36 us (5%)
    all_to_all x1, blocking collectives, sent_and_summed(): lax.all_to_all(parts, axis, split_axis=0, concat_axis=0, tiled=True)  25.5 us
    all_to_all x2, blocking collectives, copy_for_each(): return lax.all_to_all(copies, axis, split_axis=0, concat_axis=0, tiled=True)  23.6 us
    all_to_all x1, waiting for transfers between devices, copy_for_each(): return lax.all_to_all(copies, axis, split_axis=0, concat_axis=0, tiled=True)  16.6 us
    all_to_all x1, starting transfers between devices, summed_on_arrival(): parts = lax.all_to_all(split_up(value, dim, size), axis, 0, 0, tiled=True)  7.52 us
    all_to_all x1, waiting for transfers between devices, summed_on_arrival(): parts = lax.all_to_all(split_up(value, dim, size), axis, 0, 0, tiled=True)  6.93 us
    dot_general x1, matrix products, local(): jnp.dot(integrals, gather_directly(shares, PAIR, 0), preferred_element_ty...  6.65 us
    reshape x1, matrix products, split_up(): value.reshape(*lengths[:dim], size, lengths[dim] // size, *lengths[dim +...  6.48 us
    all_to_all x1, starting transfers between devices, copy_for_each(): return lax.all_to_all(copies, axis, split_axis=0, concat_axis=0, tiled=True)  3.89 us
  transfers between devices with their start and end apart: 2, of which 2 were waited for; matrix products, arithmetic and copies ran while one was open for 1% of the time, Pallas kernels for 0%

commit v1 on v0

v1 whole, which is shorter than its diff:
```python
import functools

import jax
import jax.numpy as jnp
from jax import lax
from jax.experimental import pallas as pl
from jax.experimental.pallas import tpu as pltpu
from jax.sharding import Mesh
from jax.sharding import PartitionSpec as P

AXES = ("z", "x", "y", "c")
PAIR = ("z", "x")
AUX = ("y", "c")
EPSILON = 1e-06
PIECES = 4
F32 = jnp.float32
BF16 = jnp.bfloat16
NT = (((1,), (1,)), ((), ()))


def far_first(i, n):
    step = lax.div(i + 1, 2)
    return n // 2 + step * (1 - 2 * lax.rem(i, 2))


def kernel(
    sizes,
    integrals,
    gaps,
    trial,
    sigma,
    subspace,
    residuals,
    norms,
    held,
    v,
    g,
    vh,
    parts,
    parts_in,
    half,
    at,
    mx,
    mz,
    gram_out,
    gram_in,
    prows,
    terms,
    terms_in,
    naux,
    npair,
    sig,
    res,
    load_sem,
    small_load,
    out_sem,
    send_sem,
    recv_sem,
):
    nz, nx, ny, nc = sizes
    na, npairs = ny * nc, nz * nx
    vectors, rows = v.shape
    columns = held.shape[1]
    kz, cx = vectors // nz, columns // nx
    own, ka = rows // na, vectors // na
    total_pairs = float(rows * npairs)
    z, x, y, c = (lax.axis_index(n) for n in AXES)
    a = y * nc + c
    me = z * nx + x

    def pair_at(oz, ox):
        return {"z": lax.rem(z + oz, nz), "x": lax.rem(x + ox, nx), "y": y, "c": c}

    def aux_at(oy, oc):
        return {"z": z, "x": x, "y": lax.rem(y + oy, ny), "c": lax.rem(c + oc, nc)}

    def pair_far(t):
        return pair_at(far_first(lax.div(t, nx), nz), far_first(lax.rem(t, nx), nx))

    def aux_far(t):
        return aux_at(far_first(lax.div(t, nc), ny), far_first(lax.rem(t, nc), nc))

    def send(src, dst, k, to):
        pltpu.make_async_remote_copy(
            src_ref=src,
            dst_ref=dst,
            send_sem=send_sem.at[k],
            recv_sem=recv_sem.at[k],
            device_id=to,
            device_id_type=pl.DeviceIdType.MESH,
        ).start()

    def arrived(ref, k):
        pltpu.make_async_remote_copy(
            src_ref=ref,
            dst_ref=ref,
            send_sem=send_sem.at[k],
            recv_sem=recv_sem.at[k],
            device_id=pair_at(1, 0),
            device_id_type=pl.DeviceIdType.MESH,
        ).wait_recv()

    def sent(ref, k):
        pltpu.make_async_remote_copy(
            src_ref=ref,
            dst_ref=ref,
            send_sem=send_sem.at[k],
            recv_sem=recv_sem.at[k],
            device_id=pair_at(1, 0),
            device_id_type=pl.DeviceIdType.MESH,
        ).wait_send()

    def each(n, body):
        def step(i, carry):
            body(i)
            return carry

        lax.fori_loop(0, n, step, 0)

    load_v = pltpu.make_async_copy(trial, v, small_load.at[0])
    load_g = pltpu.make_async_copy(gaps, g, small_load.at[1])
    load_v.start()
    load_g.start()

    def columns_of(i):
        xx = lax.rem(x + far_first(i, nx), nx)
        return pl.ds(pl.multiple_of(xx * cx, 128), cx)

    piece = rows // PIECES

    def load_chunk(i):
        for p in range(PIECES):
            where = (pl.ds(p * piece, piece), columns_of(i))
            pltpu.make_async_copy(integrals.at[where], held.at[where], load_sem.at[i]).start()

    each(nx, load_chunk)

    barrier = pltpu.get_barrier_semaphore()

    def greet(to):
        pl.semaphore_signal(barrier, inc=1, device_id=to, device_id_type=pl.DeviceIdType.MESH)

    each(npairs - 1, lambda t: greet(pair_far(t)))
    each(na - 1, lambda t: greet(aux_far(t)))

    load_v.wait()
    load_g.wait()
    vh[...] = v[...].astype(BF16)

    def first_product(i):
        cols = columns_of(i)
        pltpu.make_async_copy(integrals.at[:, cols], held.at[:, cols], load_sem.at[i]).wait()
        part = jnp.dot(vh[...], held[:, cols], preferred_element_type=F32)
        parts[i] = part.astype(BF16).reshape(nz, kz, cx)

        @pl.when(i == 0)
        def _():
            pl.semaphore_wait(barrier, npairs - 1 + na - 1)

        def scatter(j):
            oz = far_first(j, nz)
            zz = lax.rem(z + oz, nz)
            to = pair_at(oz, far_first(i, nx))
            t = j * nx + i
            send(parts.at[i, zz], parts_in.at[t], 0, to)

        each(jnp.where(i == nx - 1, nz - 1, nz), scatter)

    each(nx, first_product)

    first = pl.multiple_of(a * ka, ka)
    mine = v[pl.ds(first, ka), :]
    gv = v[...] * g[...]
    m1 = lax.dot_general(mine, gv, NT, precision=lax.Precision.HIGHEST, preferred_element_type=F32)
    squares = jnp.sum(mine * mine, axis=1, keepdims=True)
    mx[x] = jnp.concatenate([m1, jnp.broadcast_to(squares, (ka, vectors))], axis=1)
    each(nx - 1, lambda t: send(mx.at[x], mx.at[x], 1, pair_at(0, far_first(t, nx))))

    arrived(parts_in, 0)
    block = parts[nx - 1, z].astype(F32)
    block = block + jnp.sum(parts_in[...].astype(F32), axis=0)
    slot = x * nz + z
    half[slot] = block.astype(BF16)
    each(npairs - 1, lambda t: send(half.at[slot], half.at[slot], 2, pair_far(t)))

    arrived(mx.at[pl.ds(0, nx - 1)], 1)
    mz[z] = jnp.sum(mx[...], axis=0)
    each(nz - 1, lambda t: send(mz.at[z], mz.at[z], 3, pair_at(far_first(t, nz), 0)))

    arrived(half.at[pl.ds(0, npairs - 1)], 2)
    for i in range(nx):
        at[:, i * cx : (i + 1) * cx] = half[i * nz : (i + 1) * nz].reshape(vectors, cx)

    gram = lax.dot_general(at[...], at[...], NT, preferred_element_type=F32)
    gram = jnp.concatenate([gram, jnp.zeros((vectors, 128 - vectors), F32)], axis=1)
    gram_out[...] = gram.reshape(na, ka, 128)

    def scatter_gram(t):
        to = aux_far(t)
        send(gram_out.at[to["y"] * nc + to["c"]], gram_in.at[a], 4, to)

    each(na - 1, scatter_gram)
    gram_in[a] = gram_out[a]

    def second_product(t):
        to = aux_far(t)
        begin = pl.multiple_of((to["y"] * nc + to["c"]) * own, own)
        out = lax.dot_general(at[...], held[pl.ds(begin, own), :], NT, preferred_element_type=F32)
        terms[t] = out.astype(BF16)
        send(terms.at[t], terms_in.at[t], 5, to)

    each(na - 1, second_product)

    arrived(mz.at[pl.ds(0, nz - 1)], 3)
    arrived(gram_in.at[pl.ds(0, na - 1)], 4)
    prows[a] = jnp.sum(mz[...], axis=0) + 2.0 * jnp.sum(gram_in[...], axis=0)
    each(na - 1, lambda t: send(prows.at[a], prows.at[a], 6, aux_far(t)))

    begin = pl.multiple_of(a * own, own)
    coupled = lax.dot_general(at[...], held[pl.ds(begin, own), :], NT, preferred_element_type=F32)
    mine_at = pl.ds(pl.multiple_of(a * own, 128), own)
    own_trial = v[:, mine_at]
    gapped = own_trial * g[:, mine_at]

    arrived(prows.at[pl.ds(0, na - 1)], 6)
    products = prows[...].reshape(vectors, 128)
    row = lax.broadcasted_iota(jnp.int32, (vectors, 128), 0)
    lane = lax.broadcasted_iota(jnp.int32, (vectors, 128), 1)
    sub = products / total_pairs
    diagonal = jnp.sum(jnp.where(row == lane, sub, 0.0), axis=1, keepdims=True)
    intersection = jnp.sum(jnp.where(lane == vectors, sub, 0.0), axis=1, keepdims=True)
    rayleigh = diagonal / (intersection + EPSILON)
    subspace[...] = sub[:, :vectors]

    arrived(terms_in, 5)
    coupled = coupled + jnp.sum(terms_in[...].astype(F32), axis=0)
    sigma_own = gapped + 2.0 * coupled
    sig[...] = sigma_own
    residual = sigma_own - rayleigh * own_trial
    res[...] = residual
    squared = residual * residual
    lanes = squared[:, :128]
    for i in range(1, own // 128):
        lanes = lanes + squared[:, i * 128 : (i + 1) * 128]
    lanes = jnp.concatenate([lanes, jnp.zeros((128 - vectors, 128), F32)], axis=0)
    naux[a] = jnp.sum(lanes.T, axis=0, keepdims=True)
    each(na - 1, lambda t: send(naux.at[a], naux.at[a], 7, aux_far(t)))
    put_sigma = pltpu.make_async_copy(sig, sigma, out_sem.at[0])
    put_residuals = pltpu.make_async_copy(res, residuals, out_sem.at[1])
    put_sigma.start()
    put_residuals.start()
    arrived(naux.at[pl.ds(0, na - 1)], 7)
    npair[me] = jnp.sum(naux[...], axis=0)
    each(npairs - 1, lambda t: send(npair.at[me], npair.at[me], 8, pair_far(t)))

    sent(parts_in, 0)
    sent(mx.at[pl.ds(0, nx - 1)], 1)
    sent(half.at[pl.ds(0, npairs - 1)], 2)
    sent(mz.at[pl.ds(0, nz - 1)], 3)
    sent(gram_in.at[pl.ds(0, na - 1)], 4)
    sent(terms_in, 5)
    sent(prows.at[pl.ds(0, na - 1)], 6)
    sent(naux.at[pl.ds(0, na - 1)], 7)
    put_sigma.wait()
    put_residuals.wait()
    arrived(npair.at[pl.ds(0, npairs - 1)], 8)
    sent(npair.at[pl.ds(0, npairs - 1)], 8)
    total = jnp.sum(npair[...], axis=0) / total_pairs
    norms[...] = jnp.sqrt(total[:, :vectors] + EPSILON)


def local(sizes, integrals, energy_gaps, trial_vectors):
    nz, nx, ny, nc = sizes
    na, npairs = ny * nc, nz * nx
    rows, columns = integrals.shape
    vectors = trial_vectors.shape[1]
    kz, cx = vectors // nz, columns // nx
    own, ka = rows // na, vectors // na
    hbm = pl.BlockSpec(memory_space=pl.ANY)
    vmem = pl.BlockSpec(memory_space=pltpu.VMEM)
    sigma, subspace, residuals, norms = pl.pallas_call(
        functools.partial(kernel, sizes),
        out_shape=(
            jax.ShapeDtypeStruct((vectors, own), F32),
            jax.ShapeDtypeStruct((vectors, vectors), F32),
            jax.ShapeDtypeStruct((vectors, own), F32),
            jax.ShapeDtypeStruct((1, vectors), F32),
        ),
        in_specs=[hbm, hbm, hbm],
        out_specs=(hbm, vmem, hbm, vmem),
        scratch_shapes=[
            pltpu.VMEM((rows, columns), BF16),
            pltpu.VMEM((vectors, rows), F32),
            pltpu.VMEM((1, rows), F32),
            pltpu.VMEM((vectors, rows), BF16),
            pltpu.VMEM((nx, nz, kz, cx), BF16),
            pltpu.VMEM((npairs - 1, kz, cx), BF16),
            pltpu.VMEM((npairs, kz, cx), BF16),
            pltpu.VMEM((vectors, columns), BF16),
            pltpu.VMEM((nx, ka, 128), F32),
            pltpu.VMEM((nz, ka, 128), F32),
            pltpu.VMEM((na, ka, 128), F32),
            pltpu.VMEM((na, ka, 128), F32),
            pltpu.VMEM((na, ka, 128), F32),
            pltpu.VMEM((na - 1, vectors, own), BF16),
            pltpu.VMEM((na - 1, vectors, own), BF16),
            pltpu.VMEM((na, 1, 128), F32),
            pltpu.VMEM((npairs, 1, 128), F32),
            pltpu.VMEM((vectors, own), F32),
            pltpu.VMEM((vectors, own), F32),
            pltpu.SemaphoreType.DMA((nx,)),
            pltpu.SemaphoreType.DMA((2,)),
            pltpu.SemaphoreType.DMA((2,)),
            pltpu.SemaphoreType.DMA((9,)),
            pltpu.SemaphoreType.DMA((9,)),
        ],
        compiler_params=pltpu.CompilerParams(
            collective_id=0, has_side_effects=True, vmem_limit_bytes=60 * 1024 * 1024
        ),
        name="sigma_build",
    )(integrals, energy_gaps.reshape(1, rows), trial_vectors.T)
    return sigma.T, subspace, residuals.T, norms.reshape(vectors)


def solution(mesh):
    sizes = (8, 4, 4, 2)
    finer = Mesh(mesh.devices.reshape(sizes), AXES)
    return build(finer, sizes)


def build(finer, sizes):
    return jax.shard_map(
        functools.partial(local, sizes),
        mesh=finer,
        in_specs=(P(PAIR, AUX), P(PAIR), P(PAIR, None)),
        out_specs=(P(PAIR + AUX, None), P(), P(PAIR + AUX, None), P()),
        check_vma=False,
    )
```

time: 112 us -> 49.3 us (0.44)
  blocking collectives: 49.1 us -> 0 us
  Pallas kernels: 0 us -> 42.8 us
  waiting for transfers between devices: 23.6 us -> 0 us
  matrix products: 14.3 us -> 0 us
  starting transfers between devices: 11.4 us -> 0 us
  other arithmetic: 5.36 us -> 0 us
    all_to_all x3 -> x0, blocking collectives: 49.1 us -> none  [the longest x1 25.5 us: sent_and_summed(): lax.all_to_all(parts, axis, split_axis=0, concat_axis=0, tiled=True)]
    pallas_call x0 -> x1, Pallas kernels: none -> 42.8 us  [local(): pl.pallas_call(functools.partial(kernel, sizes), out_shape=(jax.ShapeDtyp...]
    all_to_all x2 -> x0, waiting for transfers between devices: 23.6 us -> none  [the longest x1 16.6 us: copy_for_each(): return lax.all_to_all(copies, axis, split_axis=0, concat_axis=0, tiled=True)]
    all_to_all x2 -> x0, starting transfers between devices: 11.4 us -> none  [the longest x1 7.52 us: summed_on_arrival(): parts = lax.all_to_all(split_up(value, dim, size), axis, 0, 0, tiled=True)]
    dot_general x2 -> x0, matrix products: 7.83 us -> none  [the longest x1 6.65 us: local(): jnp.dot(integrals, gather_directly(shares, PAIR, 0), preferred_element_ty...]
    reshape x1 -> x0, matrix products: 6.48 us -> none  [split_up(): value.reshape(*lengths[:dim], size, lengths[dim] // size, *lengths[dim +...]
    unnamed x8 -> x4, local copies, waits for them, and re-layouts: 1.21 us -> 5.6 us
    gather x2 -> x0, local copies, waits for them, and re-layouts: 1.61 us -> none  [the longest x1 0.81 us: local(): jnp.diagonal(products)]
  transfers between devices with their start and end apart: 2 -> 0, of which waited for: 2 -> 0; matrix products, arithmetic and copies ran while one was open for 1% -> 0% of each run, Pallas kernels for 0% -> 0%
where the time goes in v1:
time: 49.3 us; the launch traced here: 49.1 us
  Pallas kernels  42.8 us (87%)
  local copies, waits for them, and re-layouts  5.6 us (11%)
  between operations  0.64 us (1%)
    pallas_call x1, Pallas kernels, local(): pl.pallas_call(functools.partial(kernel, sizes), out_shape=(jax.ShapeDtyp...  42.8 us
    unnamed x4, local copies, waits for them, and re-layouts  5.6 us

profile of v1, /device:TPU:1, one launch (start us, length us, event | category | flops | bytes accessed | tf_op | source)
XLA Modules:
  0.0 49.1 jit_solution(2177573788070607901)
XLA Ops:
  0.6 42.8 %sigma_build.1 = (f32[64,384]{1,0:T(8,128)}, f32[64,64]{1,0:T(8,128)}, f32[64,384]{1,0:T(8,128)}, f32[1,64]{1,0:T(1,128)}) custom-call(bf16[3072,1536]{1,0:T(8,128)(2,1)} %integrals.1, f32[1,3072]{1,0:T(1,128)} %bitcast.8, f32[64,3072]{1,0:T(8,128)} %bitcast.5), custom_call_target="tpu_custom_call" | custom-call | tf_op jit(solution)/shard_map/sigma_build/pallas_call | solution.py:281
  43.5 1.5 %copy.11 = f32[384,64]{0,1:T(8,128)} copy(f32[384,64]{0,1:T(8,128)} %bitcast.7) | data formatting | bytes 196608
  45.0 1.4 %copy.12 = f32[64,64]{1,0:T(8,128)} copy(f32[64,64]{1,0:T(8,128)} %get-tuple-element.17) | data formatting | bytes 32768
  46.4 1.5 %copy.13 = f32[384,64]{0,1:T(8,128)} copy(f32[384,64]{0,1:T(8,128)} %bitcast.6) | data formatting | bytes 196608
  47.9 1.1 %copy.14 = f32[64]{0:T(128)} copy(f32[64]{0:T(128)} %bitcast.9) | data formatting | bytes 512

commit v2 on v1

v2 whole, which is shorter than its diff:
```python
import functools

import jax
import jax.numpy as jnp
from jax import lax
from jax.experimental import pallas as pl
from jax.experimental.pallas import tpu as pltpu
from jax.sharding import Mesh
from jax.sharding import PartitionSpec as P

AXES = ("z", "x", "y", "c")
PAIR = ("z", "x")
AUX = ("y", "c")
EPSILON = 1e-06
PIECES = 4
F32 = jnp.float32
BF16 = jnp.bfloat16
NT = (((1,), (1,)), ((), ()))


def farthest(n):
    return sorted(range(n), key=lambda d: -min(d, n - d))


def far_first(i, n):
    step = lax.div(i + 1, 2)
    return n // 2 + step * (1 - 2 * lax.rem(i, 2))


def kernel(
    sizes,
    integrals,
    gaps,
    trial,
    sigma,
    subspace,
    residuals,
    norms,
    held,
    v,
    g,
    vh,
    parts,
    parts_in,
    half,
    at,
    mx,
    mz,
    gc,
    gy,
    prows,
    terms,
    terms_in,
    coupled,
    nchip,
    nall,
    load_sem,
    small_load,
    terms_sem,
    send_sem,
    recv_sem,
):
    nz, nx, ny, nc = sizes
    na, npairs = ny * nc, nz * nx
    vectors, rows = v.shape
    columns = held.shape[1]
    kz, cx = vectors // nz, columns // nx
    own, ka = rows // na, vectors // na
    total_pairs = float(rows * npairs)
    z, x, y, c = (lax.axis_index(n) for n in AXES)
    a = y * nc + c
    me = z * nx + x

    zs, xs, ys, cs = ([lax.rem(p + d, n) for d in range(n)] for p, n in zip((z, x, y, c), sizes))
    plane = [(zs[i], xs[j], y, c) for i in farthest(nz) for j in farthest(nx)][:-1]
    group = [(z, x, ys[i], cs[j]) for i in farthest(ny) for j in reversed(range(nc))][:-1]
    sibling = (z, x, y, cs[1])
    y_others = [(z, x, ys[i], c) for i in farthest(ny)][:-1]
    x_others = [(z, xs[j], y, c) for j in farthest(nx)][:-1]
    z_others = [(zs[i], x, y, c) for i in farthest(nz)][:-1]

    def send(src, dst, k, to):
        pltpu.make_async_remote_copy(
            src_ref=src,
            dst_ref=dst,
            send_sem=send_sem.at[k],
            recv_sem=recv_sem.at[k],
            device_id=to,
            device_id_type=pl.DeviceIdType.MESH,
        ).start()

    def arrived(ref, k):
        pltpu.make_async_remote_copy(
            src_ref=ref,
            dst_ref=ref,
            send_sem=send_sem.at[k],
            recv_sem=recv_sem.at[k],
            device_id=sibling,
            device_id_type=pl.DeviceIdType.MESH,
        ).wait_recv()

    def sent(ref, k):
        pltpu.make_async_remote_copy(
            src_ref=ref,
            dst_ref=ref,
            send_sem=send_sem.at[k],
            recv_sem=recv_sem.at[k],
            device_id=sibling,
            device_id_type=pl.DeviceIdType.MESH,
        ).wait_send()

    def each(n, body):
        def step(i, carry):
            body(i)
            return carry

        lax.fori_loop(0, n, step, 0)

    load_v = pltpu.make_async_copy(trial, v, small_load.at[0])
    load_g = pltpu.make_async_copy(gaps, g, small_load.at[1])
    load_v.start()
    load_g.start()

    def columns_of(i):
        xx = lax.rem(x + far_first(i, nx), nx)
        return pl.ds(pl.multiple_of(xx * cx, 128), cx)

    piece = rows // PIECES

    def load_chunk(i):
        for p in range(PIECES):
            where = (pl.ds(p * piece, piece), columns_of(i))
            pltpu.make_async_copy(integrals.at[where], held.at[where], load_sem.at[i]).start()

    load_chunk(0)
    barrier = pltpu.get_barrier_semaphore()
    for to in plane + group:
        pl.semaphore_signal(barrier, inc=1, device_id=to, device_id_type=pl.DeviceIdType.MESH)
    for i in range(1, nx):
        load_chunk(i)

    load_v.wait()
    load_g.wait()
    vh[...] = v[...].astype(BF16)

    def scatter(i):
        xx = lax.rem(x + far_first(i, nx), nx)
        for j, oz in enumerate(farthest(nz)[:-1]):
            send(parts.at[i, zs[oz]], parts_in.at[j * nx + i], 0, (zs[oz], xx, y, c))

        @pl.when(i < nx - 1)
        def _():
            send(parts.at[i, z], parts_in.at[(nz - 1) * nx + i], 0, (z, xx, y, c))

    def first_product(i):
        cols = columns_of(i)
        pltpu.make_async_copy(integrals.at[:, cols], held.at[:, cols], load_sem.at[i]).wait()
        part = jnp.dot(vh[...], held[:, cols], preferred_element_type=F32)
        parts[i] = part.astype(BF16).reshape(nz, kz, cx)

        @pl.when(i == 1)
        def _():
            pl.semaphore_wait(barrier, len(plane) + len(group))
            scatter(0)

        @pl.when(i > 0)
        def _():
            scatter(i)

    each(nx, first_product)

    first = pl.multiple_of(a * ka, ka)
    mine = v[pl.ds(first, ka), :]
    gv = v[...] * g[...]
    m1 = lax.dot_general(mine, gv, NT, precision=lax.Precision.HIGHEST, preferred_element_type=F32)
    squares = jnp.sum(mine * mine, axis=1, keepdims=True)
    mx[x] = jnp.concatenate([m1, jnp.broadcast_to(squares, (ka, vectors))], axis=1)
    for to in x_others:
        send(mx.at[x], mx.at[x], 1, to)

    arrived(parts_in, 0)
    block = parts[nx - 1, z].astype(F32)
    block = block + jnp.sum(parts_in[...].astype(F32), axis=0)
    slot = x * nz + z
    half[slot] = block.astype(BF16)
    for to in plane:
        send(half.at[slot], half.at[slot], 2, to)

    arrived(mx.at[pl.ds(0, nx - 1)], 1)
    mz[z] = jnp.sum(mx[...], axis=0)
    for to in z_others:
        send(mz.at[z], mz.at[z], 3, to)

    arrived(half.at[pl.ds(0, npairs - 1)], 2)
    for i in range(nx):
        at[:, i * cx : (i + 1) * cx] = half[i * nz : (i + 1) * nz].reshape(vectors, cx)

    low = vectors // 2

    def second_product(i):
        yy = lax.rem(y + far_first(i, ny), ny)
        begin = pl.multiple_of(yy * nc * own, nc * own)
        out = lax.dot_general(at[...], held[pl.ds(begin, nc * own), :], NT, preferred_element_type=F32)
        for j in range(nc):
            terms[i, j] = out[:, j * own : (j + 1) * own].astype(BF16)

        def put(j, to):
            pltpu.make_async_remote_copy(
                src_ref=terms.at[i, j],
                dst_ref=terms_in.at[i, c],
                send_sem=send_sem.at[5],
                recv_sem=terms_sem.at[i, c],
                device_id=to,
                device_id_type=pl.DeviceIdType.MESH,
            ).start()

        @pl.when(i < ny - 1)
        def _():
            for j in range(nc):
                put(j, (z, x, yy, j))

        @pl.when(i == ny - 1)
        def _():
            put(cs[1], sibling)
            coupled[...] = jnp.where(c == 0, out[:, :own], out[:, own:])

        @pl.when(i == 0)
        def _():
            gram = lax.dot_general(at[...], at[...], NT, preferred_element_type=F32)
            gc[c] = jnp.concatenate([gram[:low], gram[low:]], axis=1)
            send(gc.at[c], gc.at[c], 4, sibling)

        @pl.when(i == ny - 2)
        def _():
            arrived(mz.at[pl.ds(0, nz - 1)], 3)
            prows[a] = jnp.sum(mz[...], axis=0)
            for to in group:
                send(prows.at[a], prows.at[a], 6, to)
            arrived(gc.at[0], 4)
            gy[y] = gc[0] + gc[1]
            for to in y_others:
                send(gy.at[y], gy.at[y], 7, to)

    each(ny, second_product)
    mine_at = pl.ds(pl.multiple_of(a * own, 128), own)
    own_trial = v[:, mine_at]

    arrived(prows.at[pl.ds(0, na - 1)], 6)
    arrived(gy.at[pl.ds(0, ny - 1)], 7)
    gram = jnp.sum(gy[...], axis=0)
    gram = jnp.concatenate([gram[:, :vectors], gram[:, vectors:]], axis=0)
    inputs = prows[...].reshape(vectors, 2 * vectors)
    sub = (inputs[:, :vectors] + 2.0 * gram) / total_pairs
    row = lax.broadcasted_iota(jnp.int32, (vectors, vectors), 0)
    lane = lax.broadcasted_iota(jnp.int32, (vectors, vectors), 1)
    diagonal = jnp.sum(jnp.where(row == lane, sub, 0.0), axis=1, keepdims=True)
    intersection = inputs[:, vectors : vectors + 1] / total_pairs
    rayleigh = diagonal / (intersection + EPSILON)
    subspace[...] = sub

    def arrived_term(i, j):
        pltpu.make_async_remote_copy(
            src_ref=terms.at[i, j],
            dst_ref=terms_in.at[i, j],
            send_sem=send_sem.at[5],
            recv_sem=terms_sem.at[i, j],
            device_id=sibling,
            device_id_type=pl.DeviceIdType.MESH,
        ).wait_recv()
        return terms_in[i, j].astype(F32)

    total = coupled[...] + arrived_term(ny - 1, cs[1])
    for i in range(ny - 1):
        for j in range(nc):
            total = total + arrived_term(i, j)

    sigma_own = own_trial * g[:, mine_at] + 2.0 * total
    sigma[...] = sigma_own
    residual = sigma_own - rayleigh * own_trial
    residuals[...] = residual
    squared = residual * residual
    lanes = squared[:, :128]
    for i in range(1, own // 128):
        lanes = lanes + squared[:, i * 128 : (i + 1) * 128]
    lanes = jnp.concatenate([lanes, jnp.zeros((128 - vectors, 128), F32)], axis=0)
    nchip[c] = jnp.sum(lanes.T, axis=0, keepdims=True)
    send(nchip.at[c], nchip.at[c], 8, sibling)

    arrived(nchip.at[0], 8)
    nall[me * ny + y] = nchip[0] + nchip[1]

    def share(t):
        zz = lax.rem(z + far_first(lax.div(t, nx), nz), nz)
        xx = lax.rem(x + far_first(lax.rem(t, nx), nx), nx)
        for k in farthest(ny)[:-1]:
            send(nall.at[me * ny + y], nall.at[me * ny + y], 9, (zz, xx, ys[k], c))

        @pl.when(t < npairs - 1)
        def _():
            send(nall.at[me * ny + y], nall.at[me * ny + y], 9, (zz, xx, y, c))

    each(npairs, share)

    sent(parts_in, 0)
    sent(mx.at[pl.ds(0, nx - 1)], 1)
    sent(half.at[pl.ds(0, npairs - 1)], 2)
    sent(mz.at[pl.ds(0, nz - 1)], 3)
    sent(gc.at[0], 4)
    sent(terms.at[pl.ds(0, ny - 1)], 5)
    sent(terms.at[0, 0], 5)
    sent(prows.at[pl.ds(0, na - 1)], 6)
    sent(gy.at[pl.ds(0, ny - 1)], 7)
    sent(nchip.at[0], 8)

    arrived(nall.at[pl.ds(0, npairs * ny - 1)], 9)
    sent(nall.at[pl.ds(0, npairs * ny - 1)], 9)
    total = jnp.sum(nall[...], axis=0) / total_pairs
    norms[...] = jnp.sqrt(total[:, :vectors] + EPSILON)


def put_out(*refs):
    copies = [pltpu.make_async_copy(refs[i], refs[4 + i], refs[8].at[i]) for i in range(4)]
    for copy in copies:
        copy.start()
    for copy in copies:
        copy.wait()


def local(sizes, integrals, energy_gaps, trial_vectors):
    nz, nx, ny, nc = sizes
    na, npairs = ny * nc, nz * nx
    rows, columns = integrals.shape
    vectors = trial_vectors.shape[1]
    kz, cx = vectors // nz, columns // nx
    own, ka = rows // na, vectors // na
    hbm = pl.BlockSpec(memory_space=pl.ANY)
    vmem = pl.BlockSpec(memory_space=pltpu.VMEM)
    shapes = ((vectors, own), (vectors, vectors), (vectors, own), (1, vectors))
    results = pl.pallas_call(
        functools.partial(kernel, sizes),
        out_shape=tuple(pltpu.VMEM(s, F32) for s in shapes),
        in_specs=[hbm, hbm, hbm],
        out_specs=(vmem,) * 4,
        scratch_shapes=[
            pltpu.VMEM((rows, columns), BF16),
            pltpu.VMEM((vectors, rows), F32),
            pltpu.VMEM((1, rows), F32),
            pltpu.VMEM((vectors, rows), BF16),
            pltpu.VMEM((nx, nz, kz, cx), BF16),
            pltpu.VMEM((npairs - 1, kz, cx), BF16),
            pltpu.VMEM((npairs, kz, cx), BF16),
            pltpu.VMEM((vectors, columns), BF16),
            pltpu.VMEM((nx, ka, 128), F32),
            pltpu.VMEM((nz, ka, 128), F32),
            pltpu.VMEM((nc, vectors // 2, 2 * vectors), F32),
            pltpu.VMEM((ny, vectors // 2, 2 * vectors), F32),
            pltpu.VMEM((na, ka, 128), F32),
            pltpu.VMEM((ny, nc, vectors, own), BF16),
            pltpu.VMEM((ny, nc, vectors, own), BF16),
            pltpu.VMEM((vectors, own), F32),
            pltpu.VMEM((nc, 1, 128), F32),
            pltpu.VMEM((npairs * ny, 1, 128), F32),
            pltpu.SemaphoreType.DMA((nx,)),
            pltpu.SemaphoreType.DMA((2,)),
            pltpu.SemaphoreType.DMA((ny, nc)),
            pltpu.SemaphoreType.DMA((10,)),
            pltpu.SemaphoreType.DMA((10,)),
        ],
        compiler_params=pltpu.CompilerParams(
            collective_id=0, has_side_effects=True, vmem_limit_bytes=60 * 1024 * 1024
        ),
        name="sigma_build",
    )(integrals, energy_gaps.reshape(1, rows), trial_vectors.T)
    sigma, subspace, residuals, norms = pl.pallas_call(
        put_out,
        out_shape=tuple(jax.ShapeDtypeStruct(s, F32) for s in shapes),
        in_specs=[vmem] * 4,
        out_specs=(hbm,) * 4,
        scratch_shapes=[pltpu.SemaphoreType.DMA((4,))],
        name="put_out",
    )(*[pltpu.with_memory_space_constraint(r, pltpu.VMEM) for r in results])
    return sigma.T, subspace, residuals.T, norms.reshape(vectors)


def solution(mesh):
    sizes = (8, 4, 4, 2)
    finer = Mesh(mesh.devices.reshape(sizes), AXES)
    return build(finer, sizes)


def build(finer, sizes):
    return jax.shard_map(
        functools.partial(local, sizes),
        mesh=finer,
        in_specs=(P(PAIR, AUX), P(PAIR), P(PAIR, None)),
        out_specs=(P(PAIR + AUX, None), P(), P(PAIR + AUX, None), P()),
        check_vma=False,
    )
```

time: 49.3 us -> 42.5 us (0.86)
  local copies, waits for them, and re-layouts: 5.6 us -> 0 us
  Pallas kernels: 42.8 us -> 41.8 us
    unnamed x4 -> x0, local copies, waits for them, and re-layouts: 5.6 us -> none
    pallas_call x1 -> x2, Pallas kernels: 42.8 us -> 41.8 us  [the longest x1 41.1 us: local(): pl.pallas_call(functools.partial(kernel, sizes), out_shape=tuple((pltpu.V...]
where the time goes in v2:
time: 42.5 us
  Pallas kernels  41.8 us (98%)
  between operations  0.64 us (2%)
    pallas_call x1, Pallas kernels, local(): pl.pallas_call(functools.partial(kernel, sizes), out_shape=tuple((pltpu.V...  41.1 us

profile of v2, /device:TPU:1, one launch (start us, length us, event | category | flops | bytes accessed | tf_op | source)
XLA Modules:
  0.0 42.5 jit_solution(8289303154640950)
XLA Ops:
  0.6 41.1 %sigma_build.1 = (f32[64,384]{1,0:T(8,128)S(1)}, f32[64,64]{1,0:T(8,128)S(1)}, f32[64,384]{1,0:T(8,128)S(1)}, f32[1,64]{1,0:T(1,128)S(1)}) custom-call(bf16[3072,1536]{1,0:T(8,128)(2,1)} %integrals.1, f32[1,3072]{1,0:T(1,128)} %bitcast.6, f32[64,3072]{1,0:T(8,128)} %bitcast.5), custom_call_target="tpu_custom_call" | custom-call | tf_op jit(solution)/shard_map/sigma_build/pallas_call | solution.py:339
  41.7 0.7 %put_out.1 = (f32[64,384]{1,0:T(8,128)}, f32[64,64]{1,0:T(8,128)}, f32[64,384]{1,0:T(8,128)}, f32[1,64]{1,0:T(1,128)}) custom-call(f32[64,384]{1,0:T(8,128)S(1)} %get-tuple-element.12.refs_0_, f32[64,64]{1,0:T(8,128)S(1)} %get-tuple-element.13.refs_1_, f32[64,384]{1,0:T(8,128)S(1)} %get-tuple-element.14.refs_2_, f32[1,64]{1,0:T(1,128)S(1)} %get-tuple-element.15.refs_3_), custom_call_target="tpu_custom_call" | custom-call | tf_op jit(solution)/shard_map/put_out/pallas_call | solution.py:374

commit v3 on v2

--- a/solution.py
+++ b/solution.py
@@ -37,6 +37,7 @@
     residuals,
     norms,
     held,
+    turned,
     v,
     g,
     vh,
@@ -51,12 +52,15 @@
     prows,
     terms,
     terms_in,
+    chip_out,
+    chip_in,
     coupled,
     nchip,
     nall,
     load_sem,
     small_load,
     terms_sem,
+    chip_sem,
     send_sem,
     recv_sem,
 ):
@@ -178,6 +182,12 @@
     for to in x_others:
         send(mx.at[x], mx.at[x], 1, to)
 
+    def turn(i):
+        block = pl.ds(pl.multiple_of(i * 128, 128), 128)
+        turned[:, block] = held[block, :].T
+
+    each(rows // 256, turn)
+
     arrived(parts_in, 0)
     block = parts[nx - 1, z].astype(F32)
     block = block + jnp.sum(parts_in[...].astype(F32), axis=0)
@@ -191,57 +201,86 @@
     for to in z_others:
         send(mz.at[z], mz.at[z], 3, to)
 
+    each(rows // 256, lambda i: turn(rows // 256 + i))
+
+    arrived(mz.at[pl.ds(0, nz - 1)], 3)
+    prows[a] = jnp.sum(mz[...], axis=0)
+    for to in group:
+        send(prows.at[a], prows.at[a], 6, to)
+
     arrived(half.at[pl.ds(0, npairs - 1)], 2)
     for i in range(nx):
         at[:, i * cx : (i + 1) * cx] = half[i * nz : (i + 1) * nz].reshape(vectors, cx)
 
     low = vectors // 2
+    gram = lax.dot_general(at[...], at[...], NT, preferred_element_type=F32)
+    gc[c] = jnp.concatenate([gram[:low], gram[low:]], axis=1)
+    send(gc.at[c], gc.at[c], 4, sibling)
+
+    def share_gram():
+        arrived(gc.at[0], 4)
+        gy[y] = gc[0] + gc[1]
+        for to in y_others:
+            send(gy.at[y], gy.at[y], 7, to)
+
+    @pl.when(c == 0)
+    def _():
+        share_gram()
+
+    def pass_on(i):
+        pltpu.make_async_remote_copy(
+            src_ref=chip_out.at[i],
+            dst_ref=chip_in.at[i],
+            send_sem=send_sem.at[10],
+            recv_sem=chip_sem.at[i],
+            device_id=sibling,
+            device_id_type=pl.DeviceIdType.MESH,
+        ).wait_recv()
+        whole = coupled[i] + chip_in[i].astype(F32)
+
+        @pl.when(i < ny - 1)
+        def _():
+            terms[i] = whole.astype(BF16)
+            pltpu.make_async_remote_copy(
+                src_ref=terms.at[i],
+                dst_ref=terms_in.at[i],
+                send_sem=send_sem.at[5],
+                recv_sem=terms_sem.at[i],
+                device_id=(z, x, lax.rem(y + far_first(i, ny), ny), c),
+                device_id_type=pl.DeviceIdType.MESH,
+            ).start()
+
+        @pl.when(i == ny - 1)
+        def _():
+            coupled[i] = whole
 
     def second_product(i):
         yy = lax.rem(y + far_first(i, ny), ny)
-        begin = pl.multiple_of(yy * nc * own, nc * own)
-        out = lax.dot_general(at[...], held[pl.ds(begin, nc * own), :], NT, preferred_element_type=F32)
-        for j in range(nc):
-            terms[i, j] = out[:, j * own : (j + 1) * own].astype(BF16)
-
-        def put(j, to):
-            pltpu.make_async_remote_copy(
-                src_ref=terms.at[i, j],
-                dst_ref=terms_in.at[i, c],
-                send_sem=send_sem.at[5],
-                recv_sem=terms_sem.at[i, c],
-                device_id=to,
-                device_id_type=pl.DeviceIdType.MESH,
-            ).start()
-
-        @pl.when(i < ny - 1)
-        def _():
-            for j in range(nc):
-                put(j, (z, x, yy, j))
-
-        @pl.when(i == ny - 1)
-        def _():
-            put(cs[1], sibling)
-            coupled[...] = jnp.where(c == 0, out[:, :own], out[:, own:])
-
-        @pl.when(i == 0)
-        def _():
-            gram = lax.dot_general(at[...], at[...], NT, preferred_element_type=F32)
-            gc[c] = jnp.concatenate([gram[:low], gram[low:]], axis=1)
-            send(gc.at[c], gc.at[c], 4, sibling)
-
-        @pl.when(i == ny - 2)
-        def _():
-            arrived(mz.at[pl.ds(0, nz - 1)], 3)
-            prows[a] = jnp.sum(mz[...], axis=0)
-            for to in group:
-                send(prows.at[a], prows.at[a], 6, to)
-            arrived(gc.at[0], 4)
-            gy[y] = gc[0] + gc[1]
-            for to in y_others:
-                send(gy.at[y], gy.at[y], 7, to)
+        begin = pl.multiple_of(yy * nc * own, 128)
+        out = jnp.dot(at[...], turned[:, pl.ds(begin, nc * own)], preferred_element_type=F32)
+        theirs = jnp.where(c == 0, out[:, own:], out[:, :own])
+        chip_out[i] = theirs.astype(BF16)
+        pltpu.make_async_remote_copy(
+            src_ref=chip_out.at[i],
+            dst_ref=chip_in.at[i],
+            send_sem=send_sem.at[10],
+            recv_sem=chip_sem.at[i],
+            device_id=sibling,
+            device_id_type=pl.DeviceIdType.MESH,
+        ).start()
+        coupled[i] = jnp.where(c == 0, out[:, :own], out[:, own:])
+
+        @pl.when(c == 0)
+        def _():
+            pass_on(i)
 
     each(ny, second_product)
+
+    @pl.when(c > 0)
+    def _():
+        share_gram()
+        each(ny, pass_on)
+
     mine_at = pl.ds(pl.multiple_of(a * own, 128), own)
     own_trial = v[:, mine_at]
 
@@ -258,21 +297,17 @@
     rayleigh = diagonal / (intersection + EPSILON)
     subspace[...] = sub
 
-    def arrived_term(i, j):
-        pltpu.make_async_remote_copy(
-            src_ref=terms.at[i, j],
-            dst_ref=terms_in.at[i, j],
+    total = coupled[ny - 1]
+    for i in range(ny - 1):
+        pltpu.make_async_remote_copy(
+            src_ref=terms.at[i],
+            dst_ref=terms_in.at[i],
             send_sem=send_sem.at[5],
-            recv_sem=terms_sem.at[i, j],
+            recv_sem=terms_sem.at[i],
             device_id=sibling,
             device_id_type=pl.DeviceIdType.MESH,
         ).wait_recv()
-        return terms_in[i, j].astype(F32)
-
-    total = coupled[...] + arrived_term(ny - 1, cs[1])
-    for i in range(ny - 1):
-        for j in range(nc):
-            total = total + arrived_term(i, j)
+        total = total + terms_in[i].astype(F32)
 
     sigma_own = own_trial * g[:, mine_at] + 2.0 * total
     sigma[...] = sigma_own
@@ -290,24 +325,24 @@
     nall[me * ny + y] = nchip[0] + nchip[1]
 
     def share(t):
-        zz = lax.rem(z + far_first(lax.div(t, nx), nz), nz)
-        xx = lax.rem(x + far_first(lax.rem(t, nx), nx), nx)
-        for k in farthest(ny)[:-1]:
-            send(nall.at[me * ny + y], nall.at[me * ny + y], 9, (zz, xx, ys[k], c))
-
-        @pl.when(t < npairs - 1)
-        def _():
-            send(nall.at[me * ny + y], nall.at[me * ny + y], 9, (zz, xx, y, c))
-
-    each(npairs, share)
+        zz = lax.rem(z + far_first(t, nz), nz)
+        spots = [(zz, xs[j], ys[k], c) for j in farthest(nx) for k in farthest(ny)]
+        for to in spots[:-1]:
+            send(nall.at[me * ny + y], nall.at[me * ny + y], 9, to)
+
+        @pl.when(t < nz - 1)
+        def _():
+            send(nall.at[me * ny + y], nall.at[me * ny + y], 9, spots[-1])
+
+    each(nz, share)
 
     sent(parts_in, 0)
     sent(mx.at[pl.ds(0, nx - 1)], 1)
     sent(half.at[pl.ds(0, npairs - 1)], 2)
     sent(mz.at[pl.ds(0, nz - 1)], 3)
     sent(gc.at[0], 4)
-    sent(terms.at[pl.ds(0, ny - 1)], 5)
-    sent(terms.at[0, 0], 5)
+    sent(terms, 5)
+    sent(chip_out, 10)
     sent(prows.at[pl.ds(0, na - 1)], 6)
     sent(gy.at[pl.ds(0, ny - 1)], 7)
     sent(nchip.at[0], 8)
@@ -343,6 +378,7 @@
         out_specs=(vmem,) * 4,
         scratch_shapes=[
             pltpu.VMEM((rows, columns), BF16),
+            pltpu.VMEM((columns, rows), BF16),
             pltpu.VMEM((vectors, rows), F32),
             pltpu.VMEM((1, rows), F32),
             pltpu.VMEM((vectors, rows), BF16),
@@ -355,16 +391,19 @@
             pltpu.VMEM((nc, vectors // 2, 2 * vectors), F32),
             pltpu.VMEM((ny, vectors // 2, 2 * vectors), F32),
             pltpu.VMEM((na, ka, 128), F32),
-            pltpu.VMEM((ny, nc, vectors, own), BF16),
-            pltpu.VMEM((ny, nc, vectors, own), BF16),
-            pltpu.VMEM((vectors, own), F32),
+            pltpu.VMEM((ny - 1, vectors, own), BF16),
+            pltpu.VMEM((ny - 1, vectors, own), BF16),
+            pltpu.VMEM((ny, vectors, own), BF16),
+            pltpu.VMEM((ny, vectors, own), BF16),
+            pltpu.VMEM((ny, vectors, own), F32),
             pltpu.VMEM((nc, 1, 128), F32),
             pltpu.VMEM((npairs * ny, 1, 128), F32),
             pltpu.SemaphoreType.DMA((nx,)),
             pltpu.SemaphoreType.DMA((2,)),
-            pltpu.SemaphoreType.DMA((ny, nc)),
-            pltpu.SemaphoreType.DMA((10,)),
-            pltpu.SemaphoreType.DMA((10,)),
+            pltpu.SemaphoreType.DMA((ny - 1,)),
+            pltpu.SemaphoreType.DMA((ny,)),
+            pltpu.SemaphoreType.DMA((11,)),
+            pltpu.SemaphoreType.DMA((11,)),
         ],
         compiler_params=pltpu.CompilerParams(
             collective_id=0, has_side_effects=True, vmem_limit_bytes=60 * 1024 * 1024

time: 42.5 us -> 40.8 us (0.960)
  Pallas kernels: 41.8 us -> 40 us
    pallas_call x1, Pallas kernels: 41.1 us -> 39.3 us  [local(): pl.pallas_call(functools.partial(kernel, sizes), out_shape=tuple((pltpu.V...]
where the time goes in v3:
time: 40.8 us; the launch traced here: 40.7 us
  Pallas kernels  40 us (98%)
  between operations  0.64 us (2%)
    pallas_call x1, Pallas kernels, local(): pl.pallas_call(functools.partial(kernel, sizes), out_shape=tuple((pltpu.V...  39.3 us

profile of v3, /device:TPU:1, one launch (start us, length us, event | category | flops | bytes accessed | tf_op | source)
XLA Modules:
  0.0 40.7 jit_solution(13773435644501039074)
XLA Ops:
  0.6 39.3 %sigma_build.1 = (f32[64,384]{1,0:T(8,128)S(1)}, f32[64,64]{1,0:T(8,128)S(1)}, f32[64,384]{1,0:T(8,128)S(1)}, f32[1,64]{1,0:T(1,128)S(1)}) custom-call(bf16[3072,1536]{1,0:T(8,128)(2,1)} %integrals.1, f32[1,3072]{1,0:T(1,128)} %bitcast.6, f32[64,3072]{1,0:T(8,128)} %bitcast.5), custom_call_target="tpu_custom_call" | custom-call | tf_op jit(solution)/shard_map/sigma_build/pallas_call | solution.py:374
  40.0 0.7 %put_out.1 = (f32[64,384]{1,0:T(8,128)}, f32[64,64]{1,0:T(8,128)}, f32[64,384]{1,0:T(8,128)}, f32[1,64]{1,0:T(1,128)}) custom-call(f32[64,384]{1,0:T(8,128)S(1)} %get-tuple-element.12.refs_0_, f32[64,64]{1,0:T(8,128)S(1)} %get-tuple-element.13.refs_1_, f32[64,384]{1,0:T(8,128)S(1)} %get-tuple-element.14.refs_2_, f32[1,64]{1,0:T(1,128)S(1)} %get-tuple-element.15.refs_3_), custom_call_target="tpu_custom_call" | custom-call | tf_op jit(solution)/shard_map/put_out/pallas_call | solution.py:413

commit v4 on v3

--- a/solution.py
+++ b/solution.py
@@ -13,6 +13,7 @@
 AUX = ("y", "c")
 EPSILON = 1e-06
 PIECES = 4
+HALVES = 2
 F32 = jnp.float32
 BF16 = jnp.bfloat16
 NT = (((1,), (1,)), ((), ()))
@@ -134,7 +135,8 @@
     def load_chunk(i):
         for p in range(PIECES):
             where = (pl.ds(p * piece, piece), columns_of(i))
-            pltpu.make_async_copy(integrals.at[where], held.at[where], load_sem.at[i]).start()
+            sem = load_sem.at[i, p * HALVES // PIECES]
+            pltpu.make_async_copy(integrals.at[where], held.at[where], sem).start()
 
     load_chunk(0)
     barrier = pltpu.get_barrier_semaphore()
@@ -158,8 +160,12 @@
 
     def first_product(i):
         cols = columns_of(i)
-        pltpu.make_async_copy(integrals.at[:, cols], held.at[:, cols], load_sem.at[i]).wait()
-        part = jnp.dot(vh[...], held[:, cols], preferred_element_type=F32)
+        part = 0.0
+        for h in range(HALVES):
+            span = pl.ds(h * rows // HALVES, rows // HALVES)
+            where = (span, cols)
+            pltpu.make_async_copy(integrals.at[where], held.at[where], load_sem.at[i, h]).wait()
+            part = part + jnp.dot(vh[:, span], held[where], preferred_element_type=F32)
         parts[i] = part.astype(BF16).reshape(nz, kz, cx)
 
         @pl.when(i == 1)
@@ -188,6 +194,11 @@
 
     each(rows // 256, turn)
 
+    arrived(mx.at[pl.ds(0, nx - 1)], 1)
+    mz[z] = jnp.sum(mx[...], axis=0)
+    for to in z_others:
+        send(mz.at[z], mz.at[z], 3, to)
+
     arrived(parts_in, 0)
     block = parts[nx - 1, z].astype(F32)
     block = block + jnp.sum(parts_in[...].astype(F32), axis=0)
@@ -196,11 +207,6 @@
     for to in plane:
         send(half.at[slot], half.at[slot], 2, to)
 
-    arrived(mx.at[pl.ds(0, nx - 1)], 1)
-    mz[z] = jnp.sum(mx[...], axis=0)
-    for to in z_others:
-        send(mz.at[z], mz.at[z], 3, to)
-
     each(rows // 256, lambda i: turn(rows // 256 + i))
 
     arrived(mz.at[pl.ds(0, nz - 1)], 3)
@@ -213,19 +219,17 @@
         at[:, i * cx : (i + 1) * cx] = half[i * nz : (i + 1) * nz].reshape(vectors, cx)
 
     low = vectors // 2
-    gram = lax.dot_general(at[...], at[...], NT, preferred_element_type=F32)
-    gc[c] = jnp.concatenate([gram[:low], gram[low:]], axis=1)
-    send(gc.at[c], gc.at[c], 4, sibling)
+
+    def make_gram():
+        gram = lax.dot_general(at[...], at[...], NT, preferred_element_type=F32)
+        gc[c] = jnp.concatenate([gram[:low], gram[low:]], axis=1)
+        send(gc.at[c], gc.at[c], 4, sibling)
 
     def share_gram():
         arrived(gc.at[0], 4)
         gy[y] = gc[0] + gc[1]
         for to in y_others:
             send(gy.at[y], gy.at[y], 7, to)
-
-    @pl.when(c == 0)
-    def _():
-        share_gram()
 
     def pass_on(i):
         pltpu.make_async_remote_copy(
@@ -258,8 +262,8 @@
         yy = lax.rem(y + far_first(i, ny), ny)
         begin = pl.multiple_of(yy * nc * own, 128)
         out = jnp.dot(at[...], turned[:, pl.ds(begin, nc * own)], preferred_element_type=F32)
-        theirs = jnp.where(c == 0, out[:, own:], out[:, :own])
-        chip_out[i] = theirs.astype(BF16)
+        kept = c
+        chip_out[i] = jnp.where(kept == 0, out[:, own:], out[:, :own]).astype(BF16)
         pltpu.make_async_remote_copy(
             src_ref=chip_out.at[i],
             dst_ref=chip_in.at[i],
@@ -268,18 +272,27 @@
             device_id=sibling,
             device_id_type=pl.DeviceIdType.MESH,
         ).start()
-        coupled[i] = jnp.where(c == 0, out[:, :own], out[:, own:])
+        coupled[i] = jnp.where(kept == 0, out[:, :own], out[:, own:])
 
         @pl.when(c == 0)
         def _():
             pass_on(i)
+
+        @pl.when(i == 0)
+        def _():
+            make_gram()
+
+            @pl.when(c == 0)
+            def _():
+                share_gram()
 
     each(ny, second_product)
 
     @pl.when(c > 0)
     def _():
+        pass_on(0)
         share_gram()
-        each(ny, pass_on)
+        each(ny - 1, lambda i: pass_on(i + 1))
 
     mine_at = pl.ds(pl.multiple_of(a * own, 128), own)
     own_trial = v[:, mine_at]
@@ -398,7 +411,7 @@
             pltpu.VMEM((ny, vectors, own), F32),
             pltpu.VMEM((nc, 1, 128), F32),
             pltpu.VMEM((npairs * ny, 1, 128), F32),
-            pltpu.SemaphoreType.DMA((nx,)),
+            pltpu.SemaphoreType.DMA((nx, HALVES)),
             pltpu.SemaphoreType.DMA((2,)),
             pltpu.SemaphoreType.DMA((ny - 1,)),
             pltpu.SemaphoreType.DMA((ny,)),

time: 40.8 us -> 41 us (level)
  no operation moved by 1% of the time
where the time goes in v4:
time: 41 us; the launch traced here: 40.9 us
  Pallas kernels  40.3 us (98%)
  between operations  0.64 us (2%)
    pallas_call x1, Pallas kernels, local(): pl.pallas_call(functools.partial(kernel, sizes), out_shape=tuple((pltpu.V...  39.5 us

profile of v4, /device:TPU:1, one launch (start us, length us, event | category | flops | bytes accessed | tf_op | source)
XLA Modules:
  0.0 40.9 jit_solution(15842638049771484436)
XLA Ops:
  0.6 39.5 %sigma_build.1 = (f32[64,384]{1,0:T(8,128)S(1)}, f32[64,64]{1,0:T(8,128)S(1)}, f32[64,384]{1,0:T(8,128)S(1)}, f32[1,64]{1,0:T(1,128)S(1)}) custom-call(bf16[3072,1536]{1,0:T(8,128)(2,1)} %integrals.1, f32[1,3072]{1,0:T(1,128)} %bitcast.6, f32[64,3072]{1,0:T(8,128)} %bitcast.5), custom_call_target="tpu_custom_call" | custom-call | tf_op jit(solution)/shard_map/sigma_build/pallas_call | solution.py:387
  40.2 0.7 %put_out.1 = (f32[64,384]{1,0:T(8,128)}, f32[64,64]{1,0:T(8,128)}, f32[64,384]{1,0:T(8,128)}, f32[1,64]{1,0:T(1,128)}) custom-call(f32[64,384]{1,0:T(8,128)S(1)} %get-tuple-element.12.refs_0_, f32[64,64]{1,0:T(8,128)S(1)} %get-tuple-element.13.refs_1_, f32[64,384]{1,0:T(8,128)S(1)} %get-tuple-element.14.refs_2_, f32[1,64]{1,0:T(1,128)S(1)} %get-tuple-element.15.refs_3_), custom_call_target="tpu_custom_call" | custom-call | tf_op jit(solution)/shard_map/put_out/pallas_call | solution.py:426

commit v5 on v3

--- a/solution.py
+++ b/solution.py
@@ -13,6 +13,7 @@
 AUX = ("y", "c")
 EPSILON = 1e-06
 PIECES = 4
+HALVES = 2
 F32 = jnp.float32
 BF16 = jnp.bfloat16
 NT = (((1,), (1,)), ((), ()))
@@ -134,7 +135,8 @@
     def load_chunk(i):
         for p in range(PIECES):
             where = (pl.ds(p * piece, piece), columns_of(i))
-            pltpu.make_async_copy(integrals.at[where], held.at[where], load_sem.at[i]).start()
+            sem = load_sem.at[i, p * HALVES // PIECES]
+            pltpu.make_async_copy(integrals.at[where], held.at[where], sem).start()
 
     load_chunk(0)
     barrier = pltpu.get_barrier_semaphore()
@@ -158,8 +160,12 @@
 
     def first_product(i):
         cols = columns_of(i)
-        pltpu.make_async_copy(integrals.at[:, cols], held.at[:, cols], load_sem.at[i]).wait()
-        part = jnp.dot(vh[...], held[:, cols], preferred_element_type=F32)
+        part = 0.0
+        for h in range(HALVES):
+            span = pl.ds(h * rows // HALVES, rows // HALVES)
+            where = (span, cols)
+            pltpu.make_async_copy(integrals.at[where], held.at[where], load_sem.at[i, h]).wait()
+            part = part + jnp.dot(vh[:, span], held[where], preferred_element_type=F32)
         parts[i] = part.astype(BF16).reshape(nz, kz, cx)
 
         @pl.when(i == 1)
@@ -188,6 +194,11 @@
 
     each(rows // 256, turn)
 
+    arrived(mx.at[pl.ds(0, nx - 1)], 1)
+    mz[z] = jnp.sum(mx[...], axis=0)
+    for to in z_others:
+        send(mz.at[z], mz.at[z], 3, to)
+
     arrived(parts_in, 0)
     block = parts[nx - 1, z].astype(F32)
     block = block + jnp.sum(parts_in[...].astype(F32), axis=0)
@@ -195,11 +206,6 @@
     half[slot] = block.astype(BF16)
     for to in plane:
         send(half.at[slot], half.at[slot], 2, to)
-
-    arrived(mx.at[pl.ds(0, nx - 1)], 1)
-    mz[z] = jnp.sum(mx[...], axis=0)
-    for to in z_others:
-        send(mz.at[z], mz.at[z], 3, to)
 
     each(rows // 256, lambda i: turn(rows // 256 + i))
 
@@ -398,7 +404,7 @@
             pltpu.VMEM((ny, vectors, own), F32),
             pltpu.VMEM((nc, 1, 128), F32),
             pltpu.VMEM((npairs * ny, 1, 128), F32),
-            pltpu.SemaphoreType.DMA((nx,)),
+            pltpu.SemaphoreType.DMA((nx, HALVES)),
             pltpu.SemaphoreType.DMA((2,)),
             pltpu.SemaphoreType.DMA((ny - 1,)),
             pltpu.SemaphoreType.DMA((ny,)),

time: 40.8 us -> 40.8 us (level)
  no operation moved by 1% of the time
where the time goes in v5:
time: 40.8 us
  Pallas kernels  40.1 us (98%)
  between operations  0.64 us (2%)
    pallas_call x1, Pallas kernels, local(): pl.pallas_call(functools.partial(kernel, sizes), out_shape=tuple((pltpu.V...  39.4 us

profile of v5, /device:TPU:1, one launch (start us, length us, event | category | flops | bytes accessed | tf_op | source)
XLA Modules:
  0.0 40.8 jit_solution(13585475726662145514)
XLA Ops:
  0.6 39.4 %sigma_build.1 = (f32[64,384]{1,0:T(8,128)S(1)}, f32[64,64]{1,0:T(8,128)S(1)}, f32[64,384]{1,0:T(8,128)S(1)}, f32[1,64]{1,0:T(1,128)S(1)}) custom-call(bf16[3072,1536]{1,0:T(8,128)(2,1)} %integrals.1, f32[1,3072]{1,0:T(1,128)} %bitcast.6, f32[64,3072]{1,0:T(8,128)} %bitcast.5), custom_call_target="tpu_custom_call" | custom-call | tf_op jit(solution)/shard_map/sigma_build/pallas_call | solution.py:380
  40.0 0.7 %put_out.1 = (f32[64,384]{1,0:T(8,128)}, f32[64,64]{1,0:T(8,128)}, f32[64,384]{1,0:T(8,128)}, f32[1,64]{1,0:T(1,128)}) custom-call(f32[64,384]{1,0:T(8,128)S(1)} %get-tuple-element.12.refs_0_, f32[64,64]{1,0:T(8,128)S(1)} %get-tuple-element.13.refs_1_, f32[64,384]{1,0:T(8,128)S(1)} %get-tuple-element.14.refs_2_, f32[1,64]{1,0:T(1,128)S(1)} %get-tuple-element.15.refs_3_), custom_call_target="tpu_custom_call" | custom-call | tf_op jit(solution)/shard_map/put_out/pallas_call | solution.py:419

commit v6 on v5

--- a/solution.py
+++ b/solution.py
@@ -13,7 +13,7 @@
 AUX = ("y", "c")
 EPSILON = 1e-06
 PIECES = 4
-HALVES = 2
+HALVES = 4
 F32 = jnp.float32
 BF16 = jnp.bfloat16
 NT = (((1,), (1,)), ((), ()))

time: 40.8 us -> 41 us (level)
  no operation moved by 1% of the time
where the time goes in v6:
time: 41 us; the launch traced here: 40.9 us
  Pallas kernels  40.3 us (98%)
  between operations  0.64 us (2%)
    pallas_call x1, Pallas kernels, local(): pl.pallas_call(functools.partial(kernel, sizes), out_shape=tuple((pltpu.V...  39.5 us

profile of v6, /device:TPU:1, one launch (start us, length us, event | category | flops | bytes accessed | tf_op | source)
XLA Modules:
  0.0 40.9 jit_solution(12279064183799139309)
XLA Ops:
  0.6 39.5 %sigma_build.1 = (f32[64,384]{1,0:T(8,128)S(1)}, f32[64,64]{1,0:T(8,128)S(1)}, f32[64,384]{1,0:T(8,128)S(1)}, f32[1,64]{1,0:T(1,128)S(1)}) custom-call(bf16[3072,1536]{1,0:T(8,128)(2,1)} %integrals.1, f32[1,3072]{1,0:T(1,128)} %bitcast.6, f32[64,3072]{1,0:T(8,128)} %bitcast.5), custom_call_target="tpu_custom_call" | custom-call | tf_op jit(solution)/shard_map/sigma_build/pallas_call | solution.py:380
  40.2 0.7 %put_out.1 = (f32[64,384]{1,0:T(8,128)}, f32[64,64]{1,0:T(8,128)}, f32[64,384]{1,0:T(8,128)}, f32[1,64]{1,0:T(1,128)}) custom-call(f32[64,384]{1,0:T(8,128)S(1)} %get-tuple-element.12.refs_0_, f32[64,64]{1,0:T(8,128)S(1)} %get-tuple-element.13.refs_1_, f32[64,384]{1,0:T(8,128)S(1)} %get-tuple-element.14.refs_2_, f32[1,64]{1,0:T(1,128)S(1)} %get-tuple-element.15.refs_3_), custom_call_target="tpu_custom_call" | custom-call | tf_op jit(solution)/shard_map/put_out/pallas_call | solution.py:419
